TPU v7x, 256 devices: a whole 4x4x8 slice. The times are simulated.
256 devices in a mesh: vocab: 64 (over y, z, core), section: 4 (over x).
Axes of the slice: x: 4, y: 4, z: 8, core: 2. Of those that a mesh axis runs over, the one named last changes fastest.
Arguments:
- hidden: bfloat16 [4, 256, 8192], P('section', 'vocab'), may hold values from -64 to 64
- policy_head: bfloat16 [76032, 8192], P(('vocab', 'section')), may hold values from -1 to 1
- reference_head: bfloat16 [76032, 8192], P(('vocab', 'section')), may hold values from -1 to 1
- targets: int32 [4, 256], replicated, may hold values from 0 to 76031
- loss_mask: int32 [4, 256], replicated, may hold values 0 or 1
Outputs:
- token_logprob: float32 [4, 256], replicated
- token_kl: float32 [4, 256], replicated
- totals: float32 [3], replicated
All inputs are finite; a program needn't handle non-finite values.
Results may differ from a plain program's by a relative error of at most 0.0003.
Values may be sent and summed in bfloat16 or wider, within the bound.
No kernel may reach another device: no remote copies, remote signals or barrier semaphores. Data moves between devices by JAX's collectives and lax.ppermute only.
A program may use at most 128 MiB of HBM per device.

v0:
```python
import jax
import jax.numpy as jnp
from jax import lax
from jax.sharding import Mesh
from jax.sharding import PartitionSpec as P

VOCAB_SECTION = ("vocab_0", "vocab_1", "vocab_2", "section")
VOCAB = ("vocab_0", "vocab_1", "vocab_2")


def sent_to_all(array, axis):
    count = lax.axis_size(axis)
    return lax.all_to_all(
        jnp.broadcast_to(array[None], (count, *array.shape)), axis, 0, 0, tiled=True
    )


def laid_out(pieces, dim):
    dims = list(pieces.shape[1:])
    dims[dim] *= pieces.shape[0]
    return jnp.moveaxis(pieces, 0, dim).reshape(dims)


def gather_directly(array, axis, dim):
    pieces = sent_to_all(array, axis)
    return laid_out(pieces, dim)


def all_in_one(array, axis):
    leaves = jax.tree.leaves(array)
    order = sorted(range(len(leaves)), key=lambda k: -leaves[k].size)
    width = (1, *leaves[order[0]].shape)[-1]
    lines = [
        jnp.pad(leaves[k].reshape(-1), (0, -leaves[k].size % width)).reshape(-1, width)
        for k in order
    ]
    both, at, found = (lax.all_gather(jnp.concatenate(lines), axis), 0, {})
    for k, line in zip(order, lines):
        slab = both[:, at : at + len(line)].reshape(len(both), -1)
        found[k] = slab[:, : leaves[k].size].reshape(-1, *leaves[k].shape)
        at += len(line)
    numbers = iter(range(len(leaves)))
    return jax.tree.map(lambda _: found[next(numbers)], array)


def combined_by_axis(array, axes, combine):
    for axis in axes:
        pieces = all_in_one(array, axis)
        array = jax.tree.map(lambda part: part[0], pieces)
        for k in range(1, lax.axis_size(axis)):
            array = combine(array, jax.tree.map(lambda part: part[k], pieces))
    return array


def shard_moments(hidden_rows, wanted, policy_head, reference_head, offset):
    contract_dims = (((1,), (1,)), ((), ()))
    policy_logits = lax.dot_general(
        hidden_rows, policy_head, contract_dims, preferred_element_type=jnp.float32
    )
    refer_logits = lax.dot_general(
        hidden_rows, reference_head, contract_dims, preferred_element_type=jnp.float32
    )
    policy_top = jnp.max(policy_logits, axis=1)
    policy_shift = policy_logits - policy_top[:, None]
    policy_exp = jnp.exp(policy_shift)
    policy_sum = jnp.sum(policy_exp, axis=1)
    policy_first = jnp.sum(policy_exp * policy_shift, axis=1)
    policy_cross = jnp.sum(policy_exp * (policy_logits - refer_logits), axis=1)
    columns = offset + lax.broadcasted_iota(jnp.int32, (1, policy_head.shape[0]), 1)
    chosen = jnp.sum(jnp.where(wanted[:, None] == columns, policy_logits, 0.0), axis=1)
    refer_top = jnp.max(refer_logits, axis=1)
    refer_sum = jnp.sum(jnp.exp(refer_logits - refer_top[:, None]), axis=1)
    return (policy_top, policy_sum, policy_first, policy_cross, chosen, refer_top, refer_sum)


def merge_moments(earlier, later):
    top_one, sum_one, first_one, cross_one, chosen_one, rtop_one, rsum_one = earlier
    top_two, sum_two, first_two, cross_two, chosen_two, rtop_two, rsum_two = later
    policy_top = jnp.maximum(top_one, top_two)
    factor_one = jnp.exp(top_one - policy_top)
    factor_two = jnp.exp(top_two - policy_top)
    policy_sum = factor_one * sum_one + factor_two * sum_two
    policy_first = factor_one * (first_one + (top_one - policy_top) * sum_one) + factor_two * (
        first_two + (top_two - policy_top) * sum_two
    )
    policy_cross = factor_one * cross_one + factor_two * cross_two
    refer_top = jnp.maximum(rtop_one, rtop_two)
    refer_sum = rsum_one * jnp.exp(rtop_one - refer_top) + rsum_two * jnp.exp(rtop_two - refer_top)
    return (
        policy_top,
        policy_sum,
        policy_first,
        policy_cross,
        chosen_one + chosen_two,
        refer_top,
        refer_sum,
    )


def place_moments(moments, shape):
    return tuple((moment.reshape(shape) for moment in moments))


def on_device(hidden, policy_head, reference_head, targets, loss_mask):
    width = hidden.shape[2]
    offset = lax.axis_index(VOCAB_SECTION) * policy_head.shape[0]
    micro_total, token_total = targets.shape
    gathered = gather_directly(hidden, "section", 0)
    portion = lax.all_gather(gathered, VOCAB, axis=1, tiled=True)
    span = portion.shape[1]
    wanted = targets.reshape(-1)
    moments = shard_moments(portion.reshape(-1, width), wanted, policy_head, reference_head, offset)
    moments = place_moments(moments, (micro_total, span))
    local_top, local_sum, local_first, local_cross, local_chosen, local_rtop, local_rsum = moments
    policy_top, policy_sum, policy_first, policy_cross, chosen, refer_top, refer_sum = (
        combined_by_axis(
            (local_top, local_sum, local_first, local_cross, local_chosen, local_rtop, local_rsum),
            VOCAB_SECTION,
            merge_moments,
        )
    )
    policy_lse = policy_top + jnp.log(policy_sum)
    refer_lse = refer_top + jnp.log(refer_sum)
    logprob = chosen - policy_lse
    entropy = jnp.log(policy_sum) - policy_first / policy_sum
    divergence = policy_cross / policy_sum - policy_lse + refer_lse
    weights = loss_mask.astype(jnp.float32)
    scale = 1.0 / (micro_total * token_total)
    totals = (
        jnp.stack(
            [jnp.sum(weights * logprob), jnp.sum(weights * entropy), jnp.sum(weights * divergence)]
        )
        * scale
    )
    return (logprob, divergence, totals)


def solution(mesh):
    torus = Mesh(
        mesh.devices.reshape(4, 8, 2, mesh.shape["section"]),
        ("vocab_0", "vocab_1", "vocab_2", "section"),
    )
    placed = (P("section", VOCAB, None), P(VOCAB_SECTION, None), P(VOCAB_SECTION, None), P(), P())
    return jax.shard_map(
        on_device, mesh=torus, in_specs=placed, out_specs=(P(), P(), P()), check_vma=False
    )
```

profile of v0, /device:TPU:2, one launch (start us, length us, event | category | flops | bytes accessed | tf_op | source)
XLA Modules:
  0.0 223.6 jit_solution(3421117086802259031)
XLA Ops:
  7.2 0.0 copy-start.2
  7.2 0.0 all-gather.11.cloned.1.call-start
  7.2 0.9 broadcast_in_dim.15
  8.1 9.8 %all_to_all.5 = bf16[4,1,4,8192]{3,2,1,0:T(4,128)(2,1)S(1)} all-to-all(bf16[4,1,4,8192]{3,2,1,0:T(4,128)(2,1)S(1)} %broadcast_in_dim.15), channel_id=1, replica_groups=mesh['vocab_0'=4,'vocab_1'=8,'vocab_2'=2,'section'=4] {'section'}, dimensions={0} | all-to-all | bytes 524288 | tf_op jit(solution)/shard_map/all_to_all | solution.py:13
  18.0 0.9 copy.11
  18.9 0.0 all-gather.11.cloned.1.call-update
  18.9 0.0 copy-done.2
  19.0 101.4 %all-gather.11.cloned.1.call-done = bf16[4,1,256,8192]{3,0,1,2:T(4,128)(2,1)} async-done(((bf16[4,1,4,8192]{3,0,1,2:T(4,128)(2,1)}), bf16[4,1,256,8192]{3,0,1,2:T(4,128)(2,1)}) %all-gather.11.cloned.1.call-update) | async-done | bytes 16777232 | tf_op jit(solution)/shard_map/all_gather | solution.py:109
  120.3 14.7 %copy.12 = bf16[4,1,256,8192]{3,2,0,1:T(8,128)(2,1)S(1)} copy(bf16[4,1,256,8192]{3,0,1,2:T(4,128)(2,1)} %all-gather.11.cloned.1.call-done) | data formatting | bytes 33554432 | tf_op jit(solution)/shard_map/all_gather | solution.py:109
  135.0 0.0 copy-start
  135.1 15.1 %fusion.225 = (f32[1024]{0:T(1024)S(1)}, f32[1024,297]{0,1:T(8,128)S(1)}) fusion(bf16[1024,8192]{1,0:T(8,128)(2,1)S(1)} %bitcast.1128, bf16[297,8192]{1,0:T(8,128)(2,1)} %param.6), kind=kOutput, calls=%fused_computation.363 | convolution fusion | flops 4983136256 | bytes 22863872 | tf_op jit(solution)/shard_map/dot_general | solution.py:57
  150.2 0.0 copy-done
  150.2 10.4 %fusion.226 = (f32[1024]{0:T(1024)S(1)}, f32[1024,297]{0,1:T(8,128)S(1)}) fusion(bf16[1024,8192]{1,0:T(8,128)(2,1)} %bitcast.1129, bf16[297,8192]{1,0:T(8,128)(2,1)} %param.7), kind=kOutput, calls=%fused_computation.364 | convolution fusion | flops 4983136256 | bytes 22863872 | tf_op jit(solution)/shard_map/dot_general | solution.py:60
  160.6 0.7 fusion.1
  161.3 0.0 copy-start.1
  161.4 0.1 concatenate.12
  161.4 12.1 %all-gather.5 = f32[4,28,256]{2,1,0:T(8,128)S(1)} all-gather(f32[1,28,256]{2,1,0:T(8,128)S(1)} %bitcast.1130), channel_id=3, replica_groups=mesh['vocab_0'=4,'vocab_1'=8,'vocab_2'=2,'section'=4] {'vocab_0'}, dimensions={0}, use_global_device_ids=true | all-gather | bytes 143360 | tf_op jit(solution)/shard_map/all_gather | solution.py:37
  173.7 0.1 concatenate.13
  173.7 24.9 %all-gather.6 = f32[8,28,256]{2,1,0:T(8,128)S(1)} all-gather(f32[1,28,256]{2,1,0:T(8,128)S(1)} %bitcast.1131), channel_id=4, replica_groups=mesh['vocab_0'=4,'vocab_1'=8,'vocab_2'=2,'section'=4] {'vocab_1'}, dimensions={0}, use_global_device_ids=true | all-gather | bytes 258048 | tf_op jit(solution)/shard_map/all_gather | solution.py:37
  198.7 0.1 fusion.100
  198.8 0.1 concatenate.14
  198.9 1.8 all-gather.7
  200.8 0.1 concatenate.15
  200.9 12.1 %all-gather.8 = f32[4,28,256]{2,1,0:T(8,128)S(1)} all-gather(f32[1,28,256]{2,1,0:T(8,128)S(1)} %bitcast.1133), channel_id=6, replica_groups=mesh['vocab_0'=4,'vocab_1'=8,'vocab_2'=2,'section'=4] {'section'}, dimensions={0}, use_global_device_ids=true | all-gather | bytes 143360 | tf_op jit(solution)/shard_map/all_gather | solution.py:37
  213.0 0.0 copy-done.1
  213.0 1.3 multiply_reduce_fusion.2
  214.3 2.5 %maximum_multiply_fusion = f32[3]{0:T(128)} fusion(f32[1]{0:T(128)} %bitcast.120, f32[1]{0:T(128)} %bitcast.119, f32[1]{0:T(128)} %bitcast.114), kind=kLoop, calls=%fused_computation.362 | loop fusion | flops 9 | bytes 24 | tf_op jit(solution)/shard_map/mul | solution.py:130
  (21 shorter events, 0.3 us)
Async XLA Ops:
  7.2 11.8 %copy-start.2 = (s32[4,256]{1,0:T(4,128)S(1)}, s32[4,256]{1,0:T(4,128)}, u32[]{:S(2)}) copy-start(s32[4,256]{1,0:T(4,128)} %param.8) | copy-start | bytes 12292
  7.2 113.2 %all-gather.11.cloned.1.call-start = ((), (), s32[]{:S(2)}) async-start(), calls=%async_computation.1 | async-start | bytes 17039360 | tf_op jit(solution)/shard_map/all_gather | solution.py:109
  135.0 15.1 %copy-start = (bf16[4,1,256,8192]{3,2,0,1:T(8,128)(2,1)}, bf16[4,1,256,8192]{3,2,0,1:T(8,128)(2,1)S(1)}, u32[]{:S(2)}) copy-start(bf16[4,1,256,8192]{3,2,0,1:T(8,128)(2,1)S(1)} %copy.12) | copy-start | bytes 50331652
  161.3 51.7 %copy-start.1 = (s32[4,256]{1,0:T(4,128)S(1)}, s32[4,256]{1,0:T(4,128)}, u32[]{:S(2)}) copy-start(s32[4,256]{1,0:T(4,128)} %param.9) | copy-start | bytes 12292
Sparse Core Ops, SparseCore 0:
  19.0 101.2 all-gather.10
where the time goes:
time: 224 us
  waiting for transfers between devices  101 us (45%)
  blocking collectives  60.8 us (27%)
  matrix products  25.5 us (11%)
  local copies, waits for them, and re-layouts  16.9 us (8%)
  between operations  14.2 us (6%)
  other arithmetic  4.81 us (2%)
    all_gather x1, waiting for transfers between devices, on_device(): portion = lax.all_gather(gathered, VOCAB, axis=1, tiled=True)  101 us
    all_gather x4, blocking collectives, all_in_one(): both, at, found = (lax.all_gather(jnp.concatenate(lines), axis), 0, {})  50.9 us
    dot_general x1, matrix products, shard_moments(): lax.dot_general(hidden_rows, policy_head, contract_dims, preferred_elemen...  15.1 us
    all_gather x1, local copies, waits for them, and re-layouts, on_device(): portion = lax.all_gather(gathered, VOCAB, axis=1, tiled=True)  14.7 us
    dot_general x1, matrix products, shard_moments(): lax.dot_general(hidden_rows, reference_head, contract_dims, preferred_ele...  10.4 us
    all_to_all x1, blocking collectives, sent_to_all(): lax.all_to_all(jnp.broadcast_to(array[None], (count, *array.shape)), axis...  9.85 us
  transfers between devices with their start and end apart: 1, of which 1 were waited for; matrix products, arithmetic and copies ran while one was open for 0% of the time, Pallas kernels for 0%

commit v1 on v0

--- a/solution.py
+++ b/solution.py
@@ -106,7 +106,10 @@
     offset = lax.axis_index(VOCAB_SECTION) * policy_head.shape[0]
     micro_total, token_total = targets.shape
     gathered = gather_directly(hidden, "section", 0)
-    portion = lax.all_gather(gathered, VOCAB, axis=1, tiled=True)
+    size = lax.axis_size(VOCAB)
+    blocks = jnp.stack([gathered for _ in range(size)])
+    blocks = lax.all_to_all(blocks, VOCAB, split_axis=0, concat_axis=0)
+    portion = jnp.concatenate(blocks, axis=1)
     span = portion.shape[1]
     wanted = targets.reshape(-1)
     moments = shard_moments(portion.reshape(-1, width), wanted, policy_head, reference_head, offset)

time: 224 us -> 511 us (2.28)
  waiting for transfers between devices: 101 us -> 365 us
  local copies, waits for them, and re-layouts: 16.9 us -> 46.2 us
  between operations: 14.2 us -> 0.81 us
  starting transfers between devices: 0.04 us -> 12.5 us
    all_to_all x0 -> x1, waiting for transfers between devices: none -> 365 us  [on_device(): blocks = lax.all_to_all(blocks, VOCAB, split_axis=0, concat_axis=0)]
    all_gather x1 -> x0, waiting for transfers between devices: 101 us -> none  [on_device(): portion = lax.all_gather(gathered, VOCAB, axis=1, tiled=True)]
    another operation x0 -> x2, local copies, waits for them, and re-layouts: none -> 32.9 us  [the longest x1 23.7 us: on_device(): portion.reshape(-1, width)]
    all_gather x1 -> x0, local copies, waits for them, and re-layouts: 14.7 us -> none  [on_device(): portion = lax.all_gather(gathered, VOCAB, axis=1, tiled=True)]
    all_to_all x0 -> x1, starting transfers between devices: none -> 12.5 us  [on_device(): blocks = lax.all_to_all(blocks, VOCAB, split_axis=0, concat_axis=0)]
    reshape x0 -> x1, local copies, waits for them, and re-layouts: none -> 11.9 us  [on_device(): portion = jnp.concatenate(blocks, axis=1)]
where the time goes in v1:
time: 511 us; the launch traced here: 510 us
  waiting for transfers between devices  365 us (71%)
  blocking collectives  60.4 us (12%)
  local copies, waits for them, and re-layouts  46.2 us (9%)
  matrix products  20.8 us (4%)
  starting transfers between devices  12.5 us (2%)
    all_to_all x1, waiting for transfers between devices, on_device(): blocks = lax.all_to_all(blocks, VOCAB, split_axis=0, concat_axis=0)  365 us
    all_gather x4, blocking collectives, all_in_one(): both, at, found = (lax.all_gather(jnp.concatenate(lines), axis), 0, {})  50.5 us
    another operation x1, local copies, waits for them, and re-layouts, on_device(): portion.reshape(-1, width)  23.7 us
    all_to_all x1, starting transfers between devices, on_device(): blocks = lax.all_to_all(blocks, VOCAB, split_axis=0, concat_axis=0)  12.5 us
    reshape x1, local copies, waits for them, and re-layouts, on_device(): portion = jnp.concatenate(blocks, axis=1)  11.9 us
    dot_general x1, matrix products, shard_moments(): lax.dot_general(hidden_rows, reference_head, contract_dims, preferred_ele...  10.4 us
    dot_general x1, matrix products, shard_moments(): lax.dot_general(hidden_rows, policy_head, contract_dims, preferred_elemen...  10.4 us
  transfers between devices with their start and end apart: 1, of which 1 were waited for; matrix products, arithmetic and copies ran while one was open for 0% of the time, Pallas kernels for 0%

profile of v1, /device:TPU:2, one launch (start us, length us, event | category | flops | bytes accessed | tf_op | source)
XLA Modules:
  0.0 510.0 jit_solution(8937256547268223433)
XLA Ops:
  0.6 0.9 broadcast_in_dim.15
  1.5 9.8 %all_to_all.10 = bf16[4,1,4,8192]{3,2,1,0:T(4,128)(2,1)S(1)} all-to-all(bf16[4,1,4,8192]{3,2,1,0:T(4,128)(2,1)S(1)} %broadcast_in_dim.15), channel_id=1, replica_groups=mesh['vocab_0'=4,'vocab_1'=8,'vocab_2'=2,'section'=4] {'section'}, dimensions={0} | all-to-all | bytes 524288 | tf_op jit(solution)/shard_map/all_to_all | solution.py:13
  11.4 9.3 %stack.15 = bf16[64,4,4,8192]{3,2,1,0:T(4,128)(2,1)} broadcast(bf16[4,4,8192]{2,1,0:T(4,128)(2,1)S(1)} %bitcast.1129), dimensions={1,2,3} | broadcast | bytes 17039360 | tf_op jit(solution)/shard_map/stack | solution.py:110
  20.7 0.0 copy-start.1
  20.7 12.5 %all-to-all-start.1 = ((bf16[64,4,4,8192]{3,2,1,0:T(4,128)(2,1)}), bf16[64,4,4,8192]{3,2,1,0:T(4,128)(2,1)}, u32[]{:S(2)}, u32[]{:S(2)}) async-start(bf16[64,4,4,8192]{3,2,1,0:T(4,128)(2,1)} %stack.15), calls=%async_computation.1 | async-start | bytes 33554432 | tf_op jit(solution)/shard_map/all_to_all | solution.py:111
  33.2 0.0 copy-done.1
  33.2 364.6 %all-to-all-done.1 = bf16[64,4,4,8192]{3,2,1,0:T(4,128)(2,1)} async-done(((bf16[64,4,4,8192]{3,2,1,0:T(4,128)(2,1)}), bf16[64,4,4,8192]{3,2,1,0:T(4,128)(2,1)}, u32[]{:S(2)}, u32[]{:S(2)}) %all-to-all-start.1) | async-done | bytes 16777248 | tf_op jit(solution)/shard_map/all_to_all | solution.py:111
  397.8 11.9 %copy.8 = bf16[4,64,4,8192]{3,2,1,0:T(4,128)(2,1)} copy(bf16[4,64,4,8192]{3,2,0,1:T(4,128)(2,1)} %bitcast.2) | data formatting | bytes 33554432 | tf_op jit(solution)/shard_map/reshape | solution.py:112
  409.8 23.7 %reshape_reshape.3 = bf16[1024,8192]{1,0:T(8,128)(2,1)} reshape(bf16[4,64,4,8192]{3,2,1,0:T(4,128)(2,1)} %copy.8) | data formatting | bytes 33554432 | tf_op jit(solution)/shard_map/reshape;reshape | solution.py:115
  433.4 10.4 %fusion.225 = (f32[1024]{0:T(1024)S(1)}, f32[1024,297]{0,1:T(8,128)S(1)}) fusion(bf16[1024,8192]{1,0:T(8,128)(2,1)} %reshape_reshape.3, bf16[297,8192]{1,0:T(8,128)(2,1)} %param.6), kind=kOutput, calls=%fused_computation.363 | convolution fusion | flops 4983136256 | bytes 22863872 | tf_op jit(solution)/shard_map/dot_general | solution.py:57
  443.8 10.4 %fusion.226 = (f32[1024]{0:T(1024)S(1)}, f32[1024,297]{0,1:T(8,128)S(1)}) fusion(bf16[1024,8192]{1,0:T(8,128)(2,1)} %reshape_reshape.3, bf16[297,8192]{1,0:T(8,128)(2,1)} %param.7), kind=kOutput, calls=%fused_computation.364 | convolution fusion | flops 4983136256 | bytes 22863872 | tf_op jit(solution)/shard_map/dot_general | solution.py:60
  454.2 0.7 fusion.1
  454.9 0.0 copy-start
  455.0 0.1 concatenate.12
  455.1 12.0 %all-gather.4 = f32[4,28,256]{2,1,0:T(8,128)S(1)} all-gather(f32[1,28,256]{2,1,0:T(8,128)S(1)} %bitcast.1130), channel_id=2, replica_groups=mesh['vocab_0'=4,'vocab_1'=8,'vocab_2'=2,'section'=4] {'vocab_0'}, dimensions={0}, use_global_device_ids=true | all-gather | bytes 143360 | tf_op jit(solution)/shard_map/all_gather | solution.py:37
  467.2 0.1 concatenate.13
  467.3 25.3 %all-gather.5 = f32[8,28,256]{2,1,0:T(8,128)S(1)} all-gather(f32[1,28,256]{2,1,0:T(8,128)S(1)} %bitcast.1131), channel_id=3, replica_groups=mesh['vocab_0'=4,'vocab_1'=8,'vocab_2'=2,'section'=4] {'vocab_1'}, dimensions={0}, use_global_device_ids=true | all-gather | bytes 258048 | tf_op jit(solution)/shard_map/all_gather | solution.py:37
  492.7 0.1 fusion.100
  492.8 0.1 concatenate.14
  492.9 1.8 all-gather.6
  494.8 0.1 concatenate.15
  494.8 11.4 %all-gather.7 = f32[4,28,256]{2,1,0:T(8,128)S(1)} all-gather(f32[1,28,256]{2,1,0:T(8,128)S(1)} %bitcast.1133), channel_id=5, replica_groups=mesh['vocab_0'=4,'vocab_1'=8,'vocab_2'=2,'section'=4] {'section'}, dimensions={0}, use_global_device_ids=true | all-gather | bytes 143360 | tf_op jit(solution)/shard_map/all_gather | solution.py:37
  506.2 0.0 copy-done
  506.2 1.3 multiply_reduce_fusion.2
  507.6 2.5 maximum_multiply_fusion
  (21 shorter events, 0.3 us)
Async XLA Ops:
  20.7 12.5 %copy-start.1 = (s32[4,256]{1,0:T(4,128)S(1)}, s32[4,256]{1,0:T(4,128)}, u32[]{:S(2)}) copy-start(s32[4,256]{1,0:T(4,128)} %param.8) | copy-start | bytes 12292
  20.7 377.2 %all-to-all-start.1 = ((bf16[64,4,4,8192]{3,2,1,0:T(4,128)(2,1)}), bf16[64,4,4,8192]{3,2,1,0:T(4,128)(2,1)}, u32[]{:S(2)}, u32[]{:S(2)}) async-start(bf16[64,4,4,8192]{3,2,1,0:T(4,128)(2,1)} %stack.15), calls=%async_computation.1 | async-start | bytes 33554432 | tf_op jit(solution)/shard_map/all_to_all | solution.py:111
  454.9 51.3 %copy-start = (s32[4,256]{1,0:T(4,128)S(1)}, s32[4,256]{1,0:T(4,128)}, u32[]{:S(2)}) copy-start(s32[4,256]{1,0:T(4,128)} %param.9) | copy-start | bytes 12292
